TPU v7x, 32 devices: a whole 2x2x4 slice. The times are simulated.
32 devices in a mesh: row: 4 (over z), col: 8 (over y, x, core).
Axes of the slice: x: 2, y: 2, z: 4, core: 2. Of those that a mesh axis runs over, the one named last changes fastest.
Arguments:
- tiles: bfloat16 [4, 8, 128, 128, 128], P('row', 'col'), may hold values from -6 to 6
- tile_row: int32 [4, 8, 128], P('row', 'col'), may hold values from 0 to 63, as said below
- tile_col: int32 [4, 8, 128], P('row', 'col'), may hold values from 0 to 31
- tile_count: int32 [4, 8], P('row', 'col'), may hold values from 16 to 128, as said below
- query_ids: int32 [128], replicated, may hold values from 0 to 32767
- damping: float32 [128], replicated, may hold values from 0.006629126 to 0.026516505
Outputs:
- scores: float32 [32768, 128], P(('row', 'col'))
Inputs may be any that keep to these rules, and one draw needn't show every extreme that they name: `tile_count`: some device holds exactly 128 live slots; slots at or past the count hold arbitrary finite values and are ignored. `tile_row`: positions may repeat within a device; such tiles add. For every device and every col index o, the live slots name at most 4 distinct values among o * 8 to o * 8 + 7, and every device reaches 4 for some o. `query_ids`: ids may repeat.
All inputs are finite; a program needn't handle non-finite values.
Results may differ from a plain program's by a relative error of at most 0.003.
Values may be sent and summed in bfloat16 or wider, within the bound.
A program may use at most 128 MiB of HBM per device.

v0:
```python
import functools

import jax
import jax.numpy as jnp
from jax import lax
from jax.experimental import pallas as pl
from jax.experimental.pallas import tpu as pltpu
from jax.sharding import PartitionSpec as P

BPD = 8
TERMS = 4
TOUCH = 4
GROUPS = 4
UNROLL = 64
MESH = pl.DeviceIdType.MESH


def plan(rows, cols, count, n_col, me_col):
    slots = rows.shape[0]
    row_blocks = BPD * n_col
    slot = jnp.arange(slots, dtype=jnp.int32)
    key = jnp.where(slot < count, rows, row_blocks)
    before = (key[None, :] < key[:, None]) | ((key[None, :] == key[:, None]) & (slot[None, :] < slot[:, None]))
    rank = jnp.sum(before.astype(jnp.int32), axis=1)
    at = (rank[None, :] == slot[:, None]).astype(jnp.int32)
    perm = jnp.sum(at * slot[None, :], axis=1)
    scol = jnp.sum(at * cols[None, :], axis=1)
    same = (key[None, :] == key[:, None]) & (slot[None, :] < slot[:, None])
    cont_of = jnp.any(same, axis=1).astype(jnp.int32)
    cont = jnp.sum(at * cont_of[None, :], axis=1)
    blocks = jnp.arange(row_blocks, dtype=jnp.int32)
    hits = key[None, :] == blocks[:, None]
    marked = jnp.any(hits, axis=1).reshape(n_col, BPD)
    last = (jnp.sum((key[None, :] <= blocks[:, None]).astype(jnp.int32), axis=1) - 1).reshape(n_col, BPD)
    local = jnp.arange(BPD, dtype=jnp.int32)
    earlier = marked[:, None, :] & (local[None, None, :] < local[None, :, None])
    place = jnp.sum(earlier.astype(jnp.int32), axis=2)
    places = jnp.arange(TOUCH, dtype=jnp.int32)
    select = marked[:, None, :] & (place[:, None, :] == places[None, :, None])
    ends = jnp.sum(select.astype(jnp.int32) * last[:, None, :], axis=2).reshape(n_col * TOUCH)
    pos = jnp.where(marked, me_col * TOUCH + place, n_col * TOUCH)
    pos = jnp.pad(pos, ((0, 0), (0, 128 - BPD))).reshape(n_col, 1, 128)
    return perm, scol, cont, ends, pos


def katz_kernel(
    n_row, n_col,
    perm, scol, cont, ends,
    pos_ref, qid_ref, damp_ref, tiles_hbm,
    out_ref,
    tiles, flip, run, send, got, xbuf, total, coef, posbuf, pos_smem,
    tile_sem, pos_send, pos_recv, local_sem, send_sem, recv_sem, xsend_sem, xrecv_sem, xpass_sem,
):
    me_r = lax.axis_index("row")
    me_c = lax.axis_index("col")
    slots, tile, _ = tiles.shape
    queries = qid_ref.shape[1]
    width = queries // GROUPS

    load = pltpu.make_async_copy(tiles_hbm, tiles, tile_sem)
    load.start()
    barrier = pltpu.get_barrier_semaphore()
    for d in range(1, n_col):
        pl.semaphore_signal(barrier, inc=1, device_id=(me_r, lax.rem(me_c + d, n_col)), device_id_type=MESH)
    for d in range(1, n_row):
        pl.semaphore_signal(barrier, inc=1, device_id=(lax.rem(me_r + d, n_row), me_c), device_id_type=MESH)

    lane = lax.broadcasted_iota(jnp.int32, (queries, tile), 1)
    qid = jnp.transpose(jnp.broadcast_to(qid_ref[...], (tile, queries))) - lane
    coef[...] = jnp.transpose(jnp.broadcast_to(damp_ref[...], (tile, queries)))

    def first_x(j, carry):
        base = ((j // BPD * n_col + me_c) * BPD + lax.rem(j, BPD)) * tile
        hot = jnp.where(qid == base, 1.0, 0.0).astype(jnp.bfloat16)
        for h in range(GROUPS):
            xbuf[h][j] = hot[h * width:(h + 1) * width]
        return carry

    lax.fori_loop(0, n_row * BPD, first_x, 0)
    for t in range(TERMS * GROUPS):
        got[t][n_col * TOUCH] = jnp.zeros((width, tile), jnp.bfloat16)
    load.wait()

    def compute(t):
        def body(i, acc):
            for u in range(0, UNROLL, 2):
                p = i * UNROLL + u
                if t == 0:
                    flip[p // 2, :, :tile] = jnp.transpose(tiles[perm[p]])
                    flip[p // 2, :, tile:] = jnp.transpose(tiles[perm[p + 1]])
                both = jnp.concatenate([xbuf[t][scol[p]], xbuf[t][scol[p + 1]]], axis=0)
                prod = jnp.dot(both, flip[p // 2], preferred_element_type=jnp.float32)
                acc = jnp.where(cont[p] > 0, acc, 0.0) + prod[:width, :tile]
                run[p] = acc.astype(jnp.bfloat16)
                acc = jnp.where(cont[p + 1] > 0, acc, 0.0) + prod[width:, tile:]
                run[p + 1] = acc.astype(jnp.bfloat16)
            return acc

        lax.fori_loop(0, slots // UNROLL, body, jnp.zeros((width, tile), jnp.float32))

        def pack(s, carry):
            send[t, s] = run[ends[s]]
            return carry

        lax.fori_loop(0, n_col * TOUCH, pack, 0, unroll=n_col * TOUCH)
        for j in range(TOUCH):
            got[t][me_c * TOUCH + j] = run[ends[me_c * TOUCH + j]]

    def part_copy(t, d):
        peer = lax.rem(me_c + d, n_col)
        return pltpu.make_async_remote_copy(
            src_ref=send.at[t, pl.ds(peer * TOUCH, TOUCH)],
            dst_ref=got[t].at[pl.ds(me_c * TOUCH, TOUCH)],
            send_sem=send_sem.at[t], recv_sem=recv_sem.at[t],
            device_id=(me_r, peer), device_id_type=MESH,
        )

    def all_parts(t):
        every = pl.ds(0, (n_col - 1) * TOUCH)
        return pltpu.make_async_remote_copy(
            src_ref=send.at[t, every], dst_ref=got[t].at[every],
            send_sem=send_sem.at[t], recv_sem=recv_sem.at[t],
            device_id=(me_r, lax.rem(me_c + 1, n_col)), device_id_type=MESH,
        )

    def pos_copy(d):
        peer = lax.rem(me_c + d, n_col)
        return pltpu.make_async_remote_copy(
            src_ref=pos_ref.at[peer], dst_ref=posbuf.at[me_c],
            send_sem=pos_send.at[d], recv_sem=pos_recv.at[d],
            device_id=(me_r, peer), device_id_type=MESH,
        )

    is_end = (me_r == 0) | (me_r == n_row - 1)

    def x_rows(t, first, count, peer, sems, where):
        rows = pl.ds(first * BPD, count * BPD)
        return pltpu.make_async_remote_copy(
            src_ref=xbuf[t + GROUPS].at[rows], dst_ref=xbuf[t + GROUPS].at[rows],
            send_sem=sems.at[t, where], recv_sem=(xpass_sem if where == n_row else xrecv_sem).at[t],
            device_id=(peer, me_c), device_id_type=MESH,
        )

    def for_targets(t, act):
        order = [(lax.rem(me_r + d, n_row), d) for d in (1, n_row - 1, *range(2, n_row - 1))]
        for peer, d in order[:n_row - 1] if n_row > 2 else order[:1]:
            far = jnp.abs(peer - me_r) > 1
            skip = far & ((peer == 0) | (peer == n_row - 1))

            @pl.when(jnp.logical_not(skip))
            def _():
                act(x_rows(t, me_r, 1, peer, xsend_sem, d))

    def for_passes(t, act):
        if n_row > 2:
            @pl.when(me_r == 1)
            def _():
                act(x_rows(t, 2, n_row - 2, 0, xsend_sem, n_row))

            @pl.when(me_r == n_row - 2)
            def _():
                act(x_rows(t, 0, n_row - 2, n_row - 1, xsend_sem, n_row))

    def x_pass(t):
        @pl.when(is_end)
        def _():
            x_rows(t, 0, 1, lax.rem(me_r + 1, n_row), xsend_sem, 0).wait_recv()

        @pl.when(jnp.logical_not(is_end))
        def _():
            x_rows(t, 0, n_row - 1, lax.rem(me_r + 1, n_row), xsend_sem, 0).wait_recv()

        for_passes(t, lambda copy: copy.start())

    def x_ready(t):
        if n_row > 2:
            @pl.when(is_end)
            def _():
                x_rows(t, 0, n_row - 2, lax.rem(me_r + 1, n_row), xsend_sem, n_row).wait_recv()

    def reduce(t):
        k, h = divmod(t, GROUPS)
        all_parts(t).wait_recv()
        part = pl.ds(h * width, width)
        weight = coef[part, :]
        scale = weight
        for _ in range(k - 1):
            scale = scale * weight

        def block(b, carry):
            acc = got[t][pos_smem[0, 0, b]].astype(jnp.float32)
            for s in range(1, n_col):
                acc = acc + got[t][pos_smem[s, 0, b]].astype(jnp.float32)
            if k == 0:
                total[b, part, :] = acc
            else:
                total[b, part, :] = total[b, part, :] + scale * acc
            if k + 1 < TERMS:
                xbuf[t + GROUPS][me_r * BPD + b] = acc.astype(jnp.bfloat16)
            return carry

        lax.fori_loop(0, BPD, block, 0, unroll=BPD)
        if k + 1 < TERMS:
            for_targets(t, lambda copy: copy.start())

    steps = TERMS * GROUPS
    moves = steps - GROUPS
    for t in range(steps + 1):
        if t < steps:
            if t >= GROUPS:
                x_ready(t - GROUPS)
            compute(t)
            if t == 0:
                pl.semaphore_wait(barrier, n_col - 1 + n_row - 1)
                for d in range(1, n_col):
                    pos_copy(d).start()
            for d in range(1, n_col):
                part_copy(t, d).start()
            if t == 1:
                own = pltpu.make_async_copy(pos_ref.at[me_c], posbuf.at[me_c], local_sem)
                own.start()
                own.wait()
                for d in range(1, n_col):
                    pos_copy(d).wait_recv()
                spill = pltpu.make_async_copy(posbuf, pos_smem, local_sem)
                spill.start()
                spill.wait()
        if t >= 1:
            reduce(t - 1)
        if 2 <= t < moves + 2:
            x_pass(t - 2)

    for b in range(BPD):
        out_ref[pl.ds(b * tile, tile), :] = jnp.transpose(total[b])
    for d in range(1, n_col):
        pos_copy(d).wait_send()
    for t in range(steps):
        all_parts(t).wait_send()
    for t in range(moves):
        for_targets(t, lambda copy: copy.wait_send())
        for_passes(t, lambda copy: copy.wait_send())


def shards(tiles, tile_row, tile_col, tile_count, query_ids, damping):
    tile_block = tiles[0, 0]
    slots, tile, _ = tile_block.shape
    queries = query_ids.shape[0]
    n_row = lax.axis_size("row")
    n_col = lax.axis_size("col")
    me_col = lax.axis_index("col")
    perm, scol, cont, ends, pos = plan(tile_row[0, 0], tile_col[0, 0], tile_count[0, 0], n_col, me_col)
    width = queries // GROUPS
    steps = TERMS * GROUPS
    moves = steps - GROUPS
    bf16 = jnp.bfloat16
    dma = pltpu.SemaphoreType.DMA
    smem = pl.BlockSpec(memory_space=pltpu.SMEM)
    vmem = pl.BlockSpec(memory_space=pltpu.VMEM)
    return pl.pallas_call(
        functools.partial(katz_kernel, n_row, n_col),
        out_shape=jax.ShapeDtypeStruct((BPD * tile, queries), jnp.float32),
        in_specs=[smem] * 4 + [vmem] * 3 + [pl.BlockSpec(memory_space=pl.ANY)],
        out_specs=vmem,
        scratch_shapes=[
            pltpu.VMEM((slots, tile, tile), bf16),
            pltpu.VMEM((slots // 2, tile, 2 * tile), bf16),
            pltpu.VMEM((slots, width, tile), bf16),
            pltpu.VMEM((steps, n_col * TOUCH, width, tile), bf16),
            [pltpu.VMEM((n_col * TOUCH + 1, width, tile), bf16)] * steps,
            [pltpu.VMEM((n_row * BPD, width, tile), bf16)] * steps,
            pltpu.VMEM((BPD, queries, tile), jnp.float32),
            pltpu.VMEM((queries, tile), jnp.float32),
            pltpu.VMEM((n_col, 1, 128), jnp.int32),
            pltpu.SMEM((n_col, 1, 128), jnp.int32),
            dma, dma((n_col,)), dma((n_col,)), dma,
            dma((steps,)), dma((steps,)),
            dma((moves, n_row + 1)), dma((moves,)), dma((moves,)),
        ],
        compiler_params=pltpu.CompilerParams(
            collective_id=0, has_side_effects=True, vmem_limit_bytes=60 * 1024 * 1024
        ),
    )(perm, scol, cont, ends, pos, query_ids.reshape(1, queries), damping.reshape(1, queries), tile_block)


def solution(mesh):
    in_specs = (
        P("row", "col", None, None, None),
        P("row", "col", None),
        P("row", "col", None),
        P("row", "col"),
        P(),
        P(),
    )
    out_specs = P(("row", "col"), None)
    return jax.shard_map(shards, mesh=mesh, in_specs=in_specs, out_specs=out_specs, check_vma=False)
```

profile of v0, /device:TPU:0, one launch (start us, length us, event | category | flops | bytes accessed | tf_op | source)
XLA Modules:
  0.0 83.8 jit_solution(17302500833217831440)
XLA Ops:
  0.7 0.7 compare_select_fusion
  1.3 0.1 convert_reduce_fusion.1
  1.4 0.1 fusion.2
  1.5 0.1 and.29
  1.6 0.2 fusion.1
  1.8 0.2 convert_reduce_fusion
  2.0 1.4 %select_reduce_fusion = (s32[128]{0:T(128)}, s32[128]{0:T(128)}, s32[128]{0:T(128)}) fusion(s32[128]{0:T(128)S(1)} %convert_element_type.19, s32[128]{0:T(128)S(1)} %convert_reduce_fusion, s32[128]{0:T(128)} %bitcast.13), kind=kLoop, calls=%fused_computation | loop fusion | flops 114304 | bytes 3072 | tf_op jit(solution)/shard_map/reduce_sum | solution.py:30
  3.4 0.2 convert_reduce_fusion.2
  3.7 0.6 pad.4
  4.3 0.1 sub.7
  4.3 0.1 select_reduce_fusion.3
  4.5 0.1 copy.7
  4.6 0.6 reshape.60.ends
  5.2 76.7 %shard_map.64 = f32[1024,128]{1,0:T(8,128)} custom-call(s32[128]{0:T(128)} %get-tuple-element.7.perm, s32[128]{0:T(128)} %get-tuple-element.6.scol, s32[128]{0:T(128)} %get-tuple-element.5.cont, s32[32]{0:T(128)} %reshape.60.ends, s32[8,1,128]{2,1,0:T(1,128)} %bitcast.10, s32[1,128]{1,0:T(1,128)} %bitcast.11, f32[1,128]{1,0:T(1,128)} %bitcast.12, ...), custom_call_target="tpu_custom_call" | custom-call | tf_op jit(solution)/shard_map/pallas_call | solution.py:259
  81.9 1.9 %copy.10 = f32[1024,128]{1,0:T(8,128)} copy(f32[1024,128]{1,0:T(8,128)} %shard_map.64) | data formatting | bytes 1048576
  (4 shorter events, 0.0 us)
where the time goes:
time: 84.1 us; the launch traced here: 83.8 us
  Pallas kernels  76.7 us (91%)
  local copies, waits for them, and re-layouts  3.35 us (4%)
  other arithmetic  3.03 us (4%)
    pallas_call x1, Pallas kernels, shards(): pl.pallas_call(functools.partial(katz_kernel, n_row, n_col), out_shape=ja...  76.7 us
    unnamed x1, local copies, waits for them, and re-layouts  1.87 us

commit v1 on v0

v1 whole, which is shorter than its diff:
```python
import functools

import jax
import jax.numpy as jnp
from jax import lax
from jax.experimental import pallas as pl
from jax.experimental.pallas import tpu as pltpu
from jax.sharding import PartitionSpec as P

BPD = 8
TERMS = 4
TOUCH = 4
GROUPS = 8
UNROLL = 64
CHUNKS = 8
LAG = 3
RELAY_LAG = 5
DIRECT = GROUPS
MESH = pl.DeviceIdType.MESH


def plan(rows, cols, count, n_col, me_col):
    slots = rows.shape[1]
    row_blocks = BPD * n_col
    square = (slots, slots)
    lane = lax.broadcasted_iota(jnp.int32, square, 1)
    sub = lax.broadcasted_iota(jnp.int32, square, 0)

    def across(row):
        return jnp.broadcast_to(row, square)

    def down(row):
        return jnp.transpose(jnp.broadcast_to(row, square))

    def total(mask, value=1):
        return jnp.sum(jnp.where(mask, value, 0), axis=0, keepdims=True)

    key = jnp.where(lane[:1] < count, rows, row_blocks)
    key_l, key_s = across(key), down(key)
    twin = (key_s == key_l) & (sub < lane)
    rank = total((key_s < key_l) | twin)
    again = jnp.minimum(total(twin), 1)
    packed = lane[:1] + slots * (again + 2 * cols)
    ordered = total(down(rank) == lane, down(packed))
    perm = lax.rem(ordered, slots)
    rest = lax.div(ordered, slots)
    cont = lax.rem(rest, 2)
    scol = lax.div(rest, 2)

    marked = jnp.minimum(total(key_s == lane), 1)
    marked = jnp.where(lane[:1] < row_blocks, marked, 0)
    last = total(key_s <= lane) - 1
    owner_l = lax.div(lane[:1], BPD)
    first = owner_l * BPD
    place = total((sub >= across(first)) & (sub < lane), down(marked))
    slot_of = jnp.where(marked > 0, owner_l * TOUCH + place, -1)
    ends = total(down(slot_of) == lane, down(last))
    pos = jnp.where(marked > 0, me_col * TOUCH + place, n_col * TOUCH)
    return perm, scol, cont, ends, pos


def katz_kernel(
    n_row, n_col,
    count_ref, rows_ref, cols_ref, qid_ref, damp_ref, tiles_hbm,
    out_ref,
    tiles, flip, run, send, got, xbuf, comp, total, coef, qcol, planbuf, posbuf, poszbuf, where, order, poz,
    tile_sem, pos_send, pos_recv, posz_send, posz_recv, local_sem, send_sem, recv_sem, xsend_sem, xrecv_sem, xpass_sem,
):
    me_r = lax.axis_index("row")
    me_c = lax.axis_index("col")
    slots, tile, _ = tiles.shape
    queries = qid_ref.shape[1]
    width = queries // GROUPS
    steps = TERMS * GROUPS
    moves = steps - GROUPS
    piece = slots // CHUNKS

    def load(i):
        part = pl.ds(i * piece, piece)
        return pltpu.make_async_copy(tiles_hbm.at[part], tiles.at[part], tile_sem.at[i])

    for i in range(CHUNKS):
        load(i).start()
    barrier = pltpu.get_barrier_semaphore()
    for d in range(1, n_col):
        pl.semaphore_signal(barrier, inc=1, device_id=(me_r, lax.rem(me_c + d, n_col)), device_id_type=MESH)
    for d in range(1, n_row):
        pl.semaphore_signal(barrier, inc=1, device_id=(lax.rem(me_r + d, n_row), me_c), device_id_type=MESH)

    perm, scol, cont, ends, pos = plan(rows_ref[...], cols_ref[...], count_ref[0, 0], n_col, me_c)
    planbuf[0:1, :] = perm
    planbuf[1:2, :] = scol
    planbuf[2:3, :] = cont
    planbuf[3:4, :] = ends
    planbuf[4:5, :] = pos
    posbuf[me_c] = pos
    spill = pltpu.make_async_copy(planbuf, order, local_sem)
    spill.start()

    lane = lax.broadcasted_iota(jnp.int32, (queries, tile), 1)
    ids = qid_ref[...]
    qid = jnp.transpose(jnp.broadcast_to(ids, (tile, queries))) - lane
    coef[...] = jnp.transpose(jnp.broadcast_to(damp_ref[...], (tile, queries)))
    home = lax.rem(lax.div(ids, BPD * tile), n_col)
    qcol[...] = jnp.transpose(jnp.broadcast_to(home, (tile, queries)))

    def first_x(j, carry):
        base = ((j // BPD * n_col + me_c) * BPD + lax.rem(j, BPD)) * tile
        hot = jnp.where(qid == base, 1.0, 0.0).astype(jnp.bfloat16)
        for h in range(GROUPS):
            xbuf[h][j] = hot[h * width:(h + 1) * width]
        return carry

    lax.fori_loop(0, n_row * BPD, first_x, 0)
    for t in range(GROUPS, steps):
        got[t][n_col * TOUCH] = jnp.zeros((width, tile), jnp.bfloat16)
    for i in range(CHUNKS):
        load(i).wait()

        def turn(s, carry):
            flip[s] = jnp.transpose(tiles[s])
            return carry

        lax.fori_loop(i * piece, (i + 1) * piece, turn, 0, unroll=8)
    spill.wait()

    def compute(t):
        def body(i, acc):
            for u in range(0, UNROLL, 2):
                p = i * UNROLL + u
                weights = jnp.concatenate([flip[order[0, p]], flip[order[0, p + 1]]], axis=1)
                both = jnp.concatenate([xbuf[t][order[1, p]], xbuf[t][order[1, p + 1]]], axis=0)
                prod = jnp.dot(both, weights, preferred_element_type=jnp.float32)
                acc = jnp.where(order[2, p] > 0, acc, 0.0) + prod[:width, :tile]
                run[p] = acc.astype(jnp.bfloat16)
                acc = jnp.where(order[2, p + 1] > 0, acc, 0.0) + prod[width:, tile:]
                run[p + 1] = acc.astype(jnp.bfloat16)
            return acc

        lax.fori_loop(0, slots // UNROLL, body, jnp.zeros((width, tile), jnp.float32))
        for s in range(n_col * TOUCH):
            send[t, s] = run[order[3, s]]
        for j in range(TOUCH):
            got[t][me_c * TOUCH + j] = run[order[3, me_c * TOUCH + j]]

    def part_copy(t, d):
        peer = lax.rem(me_c + d, n_col)
        return pltpu.make_async_remote_copy(
            src_ref=send.at[t, pl.ds(peer * TOUCH, TOUCH)],
            dst_ref=got[t].at[pl.ds(me_c * TOUCH, TOUCH)],
            send_sem=send_sem.at[t], recv_sem=recv_sem.at[t],
            device_id=(me_r, peer), device_id_type=MESH,
        )

    def all_parts(t):
        every = pl.ds(0, (n_col - 1) * TOUCH)
        return pltpu.make_async_remote_copy(
            src_ref=send.at[t, every], dst_ref=got[t].at[every],
            send_sem=send_sem.at[t], recv_sem=recv_sem.at[t],
            device_id=(me_r, lax.rem(me_c + 1, n_col)), device_id_type=MESH,
        )

    def pos_copy(d):
        peer = lax.rem(me_c + d, n_col)
        return pltpu.make_async_remote_copy(
            src_ref=planbuf.at[pl.ds(4, 1)], dst_ref=posbuf.at[me_c],
            send_sem=pos_send.at[d], recv_sem=pos_recv.at[d],
            device_id=(me_r, peer), device_id_type=MESH,
        )

    def posz_copy(d):
        peer = lax.rem(me_r + d, n_row)
        return pltpu.make_async_remote_copy(
            src_ref=posbuf, dst_ref=poszbuf.at[me_r],
            send_sem=posz_send.at[d], recv_sem=posz_recv.at[d],
            device_id=(peer, me_c), device_id_type=MESH,
        )

    def unit(t, row):
        if t < GROUPS:
            return comp[t].at[pl.ds(row * TOUCH, TOUCH)]
        return xbuf[t + GROUPS].at[pl.ds(row * BPD, BPD)]

    def x_copy(t, row, peer, sem):
        return pltpu.make_async_remote_copy(
            src_ref=unit(t, row), dst_ref=unit(t, row), send_sem=sem, recv_sem=xrecv_sem.at[t, row],
            device_id=(peer, me_c), device_id_type=MESH,
        )

    is_end = (me_r == 0) | (me_r == n_row - 1)

    def for_targets(t, act):
        for far in range(n_row - 1, 0, -1):
            for way, sign in enumerate((1, -1)):
                peer = me_r + sign * far
                ok = (peer >= 0) & (peer < n_row)
                if far > 1 and t >= DIRECT:
                    ok = ok & (is_end | ((peer > 0) & (peer < n_row - 1)))

                @pl.when(ok)
                def _(far=far, way=way, peer=peer):
                    act(x_copy(t, me_r, peer, xsend_sem.at[t, 2 * far + way]))

    def passed(t):
        if n_row < 4 or t < DIRECT:
            return []
        return [(1, range(2, n_row - 1), 0), (n_row - 2, range(1, n_row - 2), n_row - 1)]

    def relay(t):
        for who, rows, end in passed(t):
            @pl.when(me_r == who)
            def _(rows=rows, end=end):
                for row in rows:
                    x_copy(t, row, end, xpass_sem.at[t, row]).wait_recv()
                    x_copy(t, row, end, xpass_sem.at[t, row]).start()

    def relay_done(t):
        for who, rows, end in passed(t):
            @pl.when(me_r == who)
            def _(rows=rows, end=end):
                for row in rows:
                    x_copy(t, row, end, xpass_sem.at[t, row]).wait_send()

    def x_ready(t):
        for row in range(n_row):
            ok = me_r != row
            for who, rows, _ in passed(t):
                if row in rows:
                    ok = ok & (me_r != who)

            @pl.when(ok)
            def _(row=row):
                x_copy(t, row, lax.rem(me_r + 1, n_row), xsend_sem.at[t, 0]).wait_recv()

    def find_places():
        def block(j, carry):
            row, b = j // BPD, lax.rem(j, BPD)
            for h in range(GROUPS):
                part = pl.ds(h * width, width)
                home_q = qcol[part, :]
                place = jnp.full((width, tile), TOUCH, jnp.int32)
                for c in range(n_col):
                    place = jnp.where(home_q == c, poz[row, c, 0, me_c * BPD + b] - c * TOUCH, place)
                where[j, part, :] = place
            return carry

        lax.fori_loop(0, n_row * BPD, block, 0, unroll=2)

    def placed(h, row, b):
        place = where[row * BPD + b, pl.ds(h * width, width), :]
        value = jnp.zeros((width, tile), jnp.float32)
        for s in range(TOUCH):
            value = jnp.where(place == s, comp[h][row * TOUCH + s].astype(jnp.float32), value)
        return value

    def expand(h):
        for row in range(n_row):
            for b in range(BPD):
                xbuf[GROUPS + h][row * BPD + b] = placed(h, row, b).astype(jnp.bfloat16)

    def keep_first(h):
        for b in range(BPD):
            total[b, pl.ds(h * width, width), :] = placed(h, me_r, b)

    def reduce(t):
        k, h = divmod(t, GROUPS)
        all_parts(t).wait_recv()
        part = pl.ds(h * width, width)
        if k == 0:
            for s in range(TOUCH):
                acc = got[t][s].astype(jnp.float32)
                for c in range(1, n_col):
                    acc = acc + got[t][c * TOUCH + s].astype(jnp.float32)
                comp[t][me_r * TOUCH + s] = acc.astype(jnp.bfloat16)
        else:
            weight = coef[part, :]
            scale = weight
            for _ in range(k - 1):
                scale = scale * weight

            def block(b, carry):
                acc = got[t][poz[me_r, 0, 0, me_c * BPD + b]].astype(jnp.float32)
                for s in range(1, n_col):
                    acc = acc + got[t][poz[me_r, s, 0, me_c * BPD + b]].astype(jnp.float32)
                total[b, part, :] = total[b, part, :] + scale * acc
                if k + 1 < TERMS:
                    xbuf[t + GROUPS][me_r * BPD + b] = acc.astype(jnp.bfloat16)
                return carry

            lax.fori_loop(0, BPD, block, 0, unroll=BPD)
        if k + 1 < TERMS:
            for_targets(t, lambda copy: copy.start())

    for t in range(steps + LAG):
        if t < steps:
            if t >= GROUPS:
                if t == GROUPS:
                    for d in range(1, n_row):
                        posz_copy(d).wait_recv()
                    table = pltpu.make_async_copy(poszbuf, poz, local_sem)
                    table.start()
                    table.wait()
                    find_places()
                x_ready(t - GROUPS)
                if t < 2 * GROUPS:
                    expand(t - GROUPS)
            compute(t)
            if t == 0:
                pl.semaphore_wait(barrier, n_col - 1 + n_row - 1)
                for d in range(1, n_col):
                    pos_copy(d).start()
            for d in range(1, n_col):
                part_copy(t, d).start()
            if GROUPS <= t < 2 * GROUPS:
                keep_first(t - GROUPS)
            if t == LAG:
                for d in range(1, n_col):
                    pos_copy(d).wait_recv()
                poszbuf[me_r] = posbuf[...]
                for d in range(1, n_row):
                    posz_copy(d).start()
        if t >= LAG:
            reduce(t - LAG)
        if 0 <= t - RELAY_LAG < moves:
            relay(t - RELAY_LAG)
        old = t - 2 * LAG - 2
        if 0 <= old:
            all_parts(old).wait_send()
            if old < moves:
                for_targets(old, lambda copy: copy.wait_send())
                relay_done(old)

    for b in range(BPD):
        out_ref[pl.ds(b * tile, tile), :] = jnp.transpose(total[b])
    for d in range(1, n_col):
        pos_copy(d).wait_send()
    for d in range(1, n_row):
        posz_copy(d).wait_send()
    for t in range(steps + LAG - 2 * LAG - 2, steps):
        all_parts(t).wait_send()


def shards(tiles, tile_row, tile_col, tile_count, query_ids, damping):
    tile_block = tiles[0, 0]
    slots, tile, _ = tile_block.shape
    queries = query_ids.shape[0]
    n_row = lax.axis_size("row")
    n_col = lax.axis_size("col")
    width = queries // GROUPS
    steps = TERMS * GROUPS
    moves = steps - GROUPS
    bf16 = jnp.bfloat16
    dma = pltpu.SemaphoreType.DMA
    smem = pl.BlockSpec(memory_space=pltpu.SMEM)
    vmem = pl.BlockSpec(memory_space=pltpu.VMEM)
    return pl.pallas_call(
        functools.partial(katz_kernel, n_row, n_col),
        out_shape=jax.ShapeDtypeStruct((BPD * tile, queries), jnp.float32),
        in_specs=[smem] + [vmem] * 4 + [pl.BlockSpec(memory_space=pl.ANY)],
        out_specs=vmem,
        scratch_shapes=[
            pltpu.VMEM((slots, tile, tile), bf16),
            pltpu.VMEM((slots, tile, tile), bf16),
            pltpu.VMEM((slots, width, tile), bf16),
            pltpu.VMEM((steps, n_col * TOUCH, width, tile), bf16),
            [pltpu.VMEM((n_col * TOUCH + 1, width, tile), bf16)] * steps,
            [pltpu.VMEM((n_row * BPD, width, tile), bf16)] * steps,
            [pltpu.VMEM((n_row * TOUCH, width, tile), bf16)] * GROUPS,
            pltpu.VMEM((BPD, queries, tile), jnp.float32),
            pltpu.VMEM((queries, tile), jnp.float32),
            pltpu.VMEM((queries, tile), jnp.int32),
            pltpu.VMEM((8, slots), jnp.int32),
            pltpu.VMEM((n_col, 1, slots), jnp.int32),
            pltpu.VMEM((n_row, n_col, 1, slots), jnp.int32),
            pltpu.VMEM((n_row * BPD, queries, tile), jnp.int32),
            pltpu.SMEM((8, slots), jnp.int32),
            pltpu.SMEM((n_row, n_col, 1, slots), jnp.int32),
            dma((CHUNKS,)), dma((n_col,)), dma((n_col,)), dma((n_row,)), dma((n_row,)), dma,
            dma((steps,)), dma((steps,)),
            dma((moves, 2 * n_row)), dma((moves, n_row)), dma((moves, n_row)),
        ],
        compiler_params=pltpu.CompilerParams(
            collective_id=0, has_side_effects=True, vmem_limit_bytes=60 * 1024 * 1024
        ),
    )(
        tile_count[:1, :1], tile_row[0], tile_col[0],
        query_ids.reshape(1, queries), damping.reshape(1, queries), tile_block,
    )


def solution(mesh):
    in_specs = (
        P("row", "col", None, None, None),
        P("row", "col", None),
        P("row", "col", None),
        P("row", "col"),
        P(),
        P(),
    )
    out_specs = P(("row", "col"), None)
    return jax.shard_map(shards, mesh=mesh, in_specs=in_specs, out_specs=out_specs, check_vma=False)
```

time: 84.1 us -> 76.7 us (0.912)
  other arithmetic: 3.03 us -> 0 us
  Pallas kernels: 76.7 us -> 74 us
  local copies, waits for them, and re-layouts: 3.35 us -> 1.87 us
    pallas_call x1, Pallas kernels: 76.7 us -> 74 us  [shards(): pl.pallas_call(functools.partial(katz_kernel, n_row, n_col), out_shape=ja...]
    reduce_sum x5 -> x0, other arithmetic: 2.05 us -> none  [the longest x1 1.39 us: plan(): cont = jnp.sum(at * cont_of[None, :], axis=1)]
where the time goes in v1:
time: 76.7 us; the launch traced here: 76.5 us
  Pallas kernels  74 us (96%)
  local copies, waits for them, and re-layouts  1.87 us (2%)
    pallas_call x1, Pallas kernels, shards(): pl.pallas_call(functools.partial(katz_kernel, n_row, n_col), out_shape=ja...  74 us
    unnamed x1, local copies, waits for them, and re-layouts  1.87 us

profile of v1, /device:TPU:0, one launch (start us, length us, event | category | flops | bytes accessed | tf_op | source)
XLA Modules:
  0.0 76.5 jit_solution(18296062676558682786)
XLA Ops:
  0.7 74.0 %shard_map.64 = f32[1024,128]{1,0:T(8,128)} custom-call(s32[1,1]{1,0:T(1,128)S(6)} %copy.8.count_ref, s32[1,128]{1,0:T(1,128)} %bitcast.6, s32[1,128]{1,0:T(1,128)} %bitcast.7, s32[1,128]{1,0:T(1,128)} %bitcast.8, f32[1,128]{1,0:T(1,128)} %bitcast.9, bf16[128,128,128]{2,1,0:T(8,128)(2,1)} %bitcast.5), custom_call_target="tpu_custom_call" | custom-call | tf_op jit(solution)/shard_map/pallas_call | solution.py:356
  74.7 1.9 %copy.9 = f32[1024,128]{1,0:T(8,128)} copy(f32[1024,128]{1,0:T(8,128)} %shard_map.64) | data formatting | bytes 1048576

commit v2 on v1

--- a/solution.py
+++ b/solution.py
@@ -11,11 +11,10 @@
 TERMS = 4
 TOUCH = 4
 GROUPS = 8
-UNROLL = 64
+UNROLL = 128
 CHUNKS = 8
-LAG = 3
-RELAY_LAG = 5
-DIRECT = GROUPS
+LAG = 2
+RELAY_LAG = 4
 MESH = pl.DeviceIdType.MESH
 
 
@@ -64,7 +63,7 @@
     count_ref, rows_ref, cols_ref, qid_ref, damp_ref, tiles_hbm,
     out_ref,
     tiles, flip, run, send, got, xbuf, comp, total, coef, qcol, planbuf, posbuf, poszbuf, where, order, poz,
-    tile_sem, pos_send, pos_recv, posz_send, posz_recv, local_sem, send_sem, recv_sem, xsend_sem, xrecv_sem, xpass_sem,
+    tile_sem, pos_send, pos_recv, posz_send, posz_recv, local_sem, send_sem, recv_sem, xsend_sem, xrecv_sem,
 ):
     me_r = lax.axis_index("row")
     me_c = lax.axis_index("col")
@@ -125,30 +124,37 @@
     spill.wait()
 
     def compute(t):
+        both = 2 * width
+
         def body(i, acc):
             for u in range(0, UNROLL, 2):
                 p = i * UNROLL + u
                 weights = jnp.concatenate([flip[order[0, p]], flip[order[0, p + 1]]], axis=1)
-                both = jnp.concatenate([xbuf[t][order[1, p]], xbuf[t][order[1, p + 1]]], axis=0)
-                prod = jnp.dot(both, weights, preferred_element_type=jnp.float32)
-                acc = jnp.where(order[2, p] > 0, acc, 0.0) + prod[:width, :tile]
+                left, right = order[1, p], order[1, p + 1]
+                x = jnp.concatenate([xbuf[t][left], xbuf[t + 1][left], xbuf[t][right], xbuf[t + 1][right]], axis=0)
+                prod = jnp.dot(x, weights, preferred_element_type=jnp.float32)
+                acc = jnp.where(order[2, p] > 0, acc, 0.0) + prod[:both, :tile]
                 run[p] = acc.astype(jnp.bfloat16)
-                acc = jnp.where(order[2, p + 1] > 0, acc, 0.0) + prod[width:, tile:]
+                acc = jnp.where(order[2, p + 1] > 0, acc, 0.0) + prod[both:, tile:]
                 run[p + 1] = acc.astype(jnp.bfloat16)
             return acc
 
-        lax.fori_loop(0, slots // UNROLL, body, jnp.zeros((width, tile), jnp.float32))
+        lax.fori_loop(0, slots // UNROLL, body, jnp.zeros((both, tile), jnp.float32))
         for s in range(n_col * TOUCH):
-            send[t, s] = run[order[3, s]]
+            value = run[order[3, s]]
+            send[t, s] = value[:width]
+            send[t + 1, s] = value[width:]
         for j in range(TOUCH):
-            got[t][me_c * TOUCH + j] = run[order[3, me_c * TOUCH + j]]
+            value = run[order[3, me_c * TOUCH + j]]
+            got[t][me_c * TOUCH + j] = value[:width]
+            got[t + 1][me_c * TOUCH + j] = value[width:]
 
     def part_copy(t, d):
         peer = lax.rem(me_c + d, n_col)
         return pltpu.make_async_remote_copy(
             src_ref=send.at[t, pl.ds(peer * TOUCH, TOUCH)],
             dst_ref=got[t].at[pl.ds(me_c * TOUCH, TOUCH)],
-            send_sem=send_sem.at[t], recv_sem=recv_sem.at[t],
+            send_sem=send_sem, recv_sem=recv_sem.at[t],
             device_id=(me_r, peer), device_id_type=MESH,
         )
 
@@ -156,7 +162,7 @@
         every = pl.ds(0, (n_col - 1) * TOUCH)
         return pltpu.make_async_remote_copy(
             src_ref=send.at[t, every], dst_ref=got[t].at[every],
-            send_sem=send_sem.at[t], recv_sem=recv_sem.at[t],
+            send_sem=send_sem, recv_sem=recv_sem.at[t],
             device_id=(me_r, lax.rem(me_c + 1, n_col)), device_id_type=MESH,
         )
 
@@ -181,76 +187,108 @@
             return comp[t].at[pl.ds(row * TOUCH, TOUCH)]
         return xbuf[t + GROUPS].at[pl.ds(row * BPD, BPD)]
 
-    def x_copy(t, row, peer, sem):
+    def relays(t):
+        if n_row < 4 or t < GROUPS:
+            return []
+        return [(1, 2, 0), (n_row - 2, 1, n_row - 1)]
+
+    def x_copy(t, first, rows, peer, sem, kind):
+        size = TOUCH if t < GROUPS else BPD
+        part = (comp[t] if t < GROUPS else xbuf[t + GROUPS]).at[pl.ds(first * size, rows * size)]
         return pltpu.make_async_remote_copy(
-            src_ref=unit(t, row), dst_ref=unit(t, row), send_sem=sem, recv_sem=xrecv_sem.at[t, row],
+            src_ref=part, dst_ref=part, send_sem=sem, recv_sem=xrecv_sem.at[t, kind],
             device_id=(peer, me_c), device_id_type=MESH,
         )
 
     is_end = (me_r == 0) | (me_r == n_row - 1)
-
-    def for_targets(t, act):
-        for far in range(n_row - 1, 0, -1):
-            for way, sign in enumerate((1, -1)):
-                peer = me_r + sign * far
-                ok = (peer >= 0) & (peer < n_row)
-                if far > 1 and t >= DIRECT:
-                    ok = ok & (is_end | ((peer > 0) & (peer < n_row - 1)))
-
-                @pl.when(ok)
-                def _(far=far, way=way, peer=peer):
-                    act(x_copy(t, me_r, peer, xsend_sem.at[t, 2 * far + way]))
-
-    def passed(t):
-        if n_row < 4 or t < DIRECT:
-            return []
-        return [(1, range(2, n_row - 1), 0), (n_row - 2, range(1, n_row - 2), n_row - 1)]
+    is_relay = (me_r == 1) | (me_r == n_row - 2)
+
+    def send_x(t):
+        for d in range(n_row - 1, 0, -1):
+            peer = lax.rem(me_r + jnp.where(2 * me_r < n_row, d, n_row - d), n_row)
+            if not relays(t):
+                x_copy(t, me_r, 1, peer, xsend_sem.at[0], 0).start()
+            else:
+                far = jnp.abs(peer - me_r) > 1
+                onward = ((peer == 1) & (me_r > 1)) | ((peer == n_row - 2) & (me_r < n_row - 2))
+                kind = jnp.where(onward & jnp.logical_not(is_end), 1, 0)
+
+                @pl.when(is_end | jnp.logical_not(far & ((peer == 0) | (peer == n_row - 1))))
+                def _(peer=peer, kind=kind):
+                    x_copy(t, me_r, 1, peer, xsend_sem.at[1], kind).start()
 
     def relay(t):
-        for who, rows, end in passed(t):
+        for who, first, end in relays(t):
             @pl.when(me_r == who)
-            def _(rows=rows, end=end):
-                for row in rows:
-                    x_copy(t, row, end, xpass_sem.at[t, row]).wait_recv()
-                    x_copy(t, row, end, xpass_sem.at[t, row]).start()
-
-    def relay_done(t):
-        for who, rows, end in passed(t):
-            @pl.when(me_r == who)
-            def _(rows=rows, end=end):
-                for row in rows:
-                    x_copy(t, row, end, xpass_sem.at[t, row]).wait_send()
+            def _(first=first, end=end):
+                x_copy(t, first, n_row - 3, end, xsend_sem.at[2], 1).wait_recv()
+                x_copy(t, first, n_row - 3, end, xsend_sem.at[2], 0).start()
 
     def x_ready(t):
-        for row in range(n_row):
-            ok = me_r != row
-            for who, rows, _ in passed(t):
-                if row in rows:
-                    ok = ok & (me_r != who)
-
-            @pl.when(ok)
-            def _(row=row):
-                x_copy(t, row, lax.rem(me_r + 1, n_row), xsend_sem.at[t, 0]).wait_recv()
+        peer = lax.rem(me_r + 1, n_row)
+        if not relays(t):
+            x_copy(t, 0, n_row - 1, peer, xsend_sem.at[0], 0).wait_recv()
+        else:
+            @pl.when(is_relay)
+            def _():
+                x_copy(t, 0, 2, peer, xsend_sem.at[1], 0).wait_recv()
+
+            @pl.when(jnp.logical_not(is_relay))
+            def _():
+                x_copy(t, 0, n_row - 1, peer, xsend_sem.at[1], 0).wait_recv()
+
+    def sent(rows, sem):
+        size = rows * width * tile
+        whole, rest = divmod(size, tile * tile)
+        assert rest == 0 and whole <= slots
+        part = tiles.at[pl.ds(0, whole)]
+        pltpu.make_async_remote_copy(
+            src_ref=part, dst_ref=part, send_sem=sem, recv_sem=xrecv_sem.at[0, 0],
+            device_id=(lax.rem(me_r + 1, n_row), me_c), device_id_type=MESH,
+        ).wait_send()
+
+    def all_x_sent():
+        sent(GROUPS * (n_row - 1) * TOUCH, xsend_sem.at[0])
+        later = (moves - GROUPS) * BPD
+        if n_row < 4:
+            sent(later * (n_row - 1), xsend_sem.at[1])
+            return
+
+        @pl.when(is_end)
+        def _():
+            sent(later * (n_row - 1), xsend_sem.at[1])
+
+        @pl.when(is_relay)
+        def _():
+            sent(later * (n_row - 2), xsend_sem.at[1])
+            sent(later * (n_row - 3), xsend_sem.at[2])
+
+        if n_row > 4:
+            @pl.when(jnp.logical_not(is_end | is_relay))
+            def _():
+                sent(later * (n_row - 3), xsend_sem.at[1])
 
     def find_places():
+        sub = lax.broadcasted_iota(jnp.int32, (n_col, tile), 0)
+        lane_c = lax.broadcasted_iota(jnp.int32, (queries, n_col), 1)
+        is_home = jnp.where(qcol[:, :n_col] == lane_c, 1.0, 0.0).astype(jnp.bfloat16)
+
         def block(j, carry):
             row, b = j // BPD, lax.rem(j, BPD)
-            for h in range(GROUPS):
-                part = pl.ds(h * width, width)
-                home_q = qcol[part, :]
-                place = jnp.full((width, tile), TOUCH, jnp.int32)
-                for c in range(n_col):
-                    place = jnp.where(home_q == c, poz[row, c, 0, me_c * BPD + b] - c * TOUCH, place)
-                where[j, part, :] = place
+            table = jnp.zeros((n_col, tile), jnp.int32)
+            for c in range(n_col):
+                table = jnp.where(sub == c, poz[row, c, 0, me_c * BPD + b] - c * TOUCH, table)
+            table = jnp.minimum(table, TOUCH).astype(jnp.float32).astype(jnp.bfloat16)
+            where[j] = jnp.dot(is_home, table, preferred_element_type=jnp.float32)
             return carry
 
-        lax.fori_loop(0, n_row * BPD, block, 0, unroll=2)
+        lax.fori_loop(0, n_row * BPD, block, 0, unroll=BPD)
 
     def placed(h, row, b):
         place = where[row * BPD + b, pl.ds(h * width, width), :]
         value = jnp.zeros((width, tile), jnp.float32)
         for s in range(TOUCH):
-            value = jnp.where(place == s, comp[h][row * TOUCH + s].astype(jnp.float32), value)
+            value = jnp.where(place == float(s), comp[h][row * TOUCH + s].astype(jnp.float32), value)
         return value
 
     def expand(h):
@@ -289,46 +327,44 @@
 
             lax.fori_loop(0, BPD, block, 0, unroll=BPD)
         if k + 1 < TERMS:
-            for_targets(t, lambda copy: copy.start())
-
-    for t in range(steps + LAG):
+            send_x(t)
+
+    for t in range(0, steps + LAG + 1, 2):
         if t < steps:
             if t >= GROUPS:
-                if t == GROUPS:
-                    for d in range(1, n_row):
-                        posz_copy(d).wait_recv()
-                    table = pltpu.make_async_copy(poszbuf, poz, local_sem)
-                    table.start()
-                    table.wait()
-                    find_places()
-                x_ready(t - GROUPS)
-                if t < 2 * GROUPS:
-                    expand(t - GROUPS)
+                for h in (t - GROUPS, t - GROUPS + 1):
+                    x_ready(h)
+                    if h < GROUPS:
+                        expand(h)
             compute(t)
             if t == 0:
                 pl.semaphore_wait(barrier, n_col - 1 + n_row - 1)
                 for d in range(1, n_col):
                     pos_copy(d).start()
-            for d in range(1, n_col):
-                part_copy(t, d).start()
-            if GROUPS <= t < 2 * GROUPS:
-                keep_first(t - GROUPS)
-            if t == LAG:
+            for h in (t, t + 1):
+                for d in range(1, n_col):
+                    part_copy(h, d).start()
+            if t == 2:
                 for d in range(1, n_col):
                     pos_copy(d).wait_recv()
                 poszbuf[me_r] = posbuf[...]
                 for d in range(1, n_row):
                     posz_copy(d).start()
-        if t >= LAG:
-            reduce(t - LAG)
-        if 0 <= t - RELAY_LAG < moves:
-            relay(t - RELAY_LAG)
-        old = t - 2 * LAG - 2
-        if 0 <= old:
-            all_parts(old).wait_send()
-            if old < moves:
-                for_targets(old, lambda copy: copy.wait_send())
-                relay_done(old)
+            if t == GROUPS - 2:
+                for d in range(1, n_row):
+                    posz_copy(d).wait_recv()
+                table = pltpu.make_async_copy(poszbuf, poz, local_sem)
+                table.start()
+                table.wait()
+                find_places()
+            if GROUPS <= t < 2 * GROUPS:
+                keep_first(t - GROUPS)
+                keep_first(t - GROUPS + 1)
+        for j in (t, t + 1):
+            if 0 <= j - LAG < steps:
+                reduce(j - LAG)
+            if 0 <= j - RELAY_LAG < moves:
+                relay(j - RELAY_LAG)
 
     for b in range(BPD):
         out_ref[pl.ds(b * tile, tile), :] = jnp.transpose(total[b])
@@ -336,8 +372,12 @@
         pos_copy(d).wait_send()
     for d in range(1, n_row):
         posz_copy(d).wait_send()
-    for t in range(steps + LAG - 2 * LAG - 2, steps):
-        all_parts(t).wait_send()
+    every = send.at[:, pl.ds(0, (n_col - 1) * TOUCH)]
+    pltpu.make_async_remote_copy(
+        src_ref=every, dst_ref=every, send_sem=send_sem, recv_sem=recv_sem.at[0],
+        device_id=(me_r, lax.rem(me_c + 1, n_col)), device_id_type=MESH,
+    ).wait_send()
+    all_x_sent()
 
 
 def shards(tiles, tile_row, tile_col, tile_count, query_ids, damping):
@@ -361,7 +401,7 @@
         scratch_shapes=[
             pltpu.VMEM((slots, tile, tile), bf16),
             pltpu.VMEM((slots, tile, tile), bf16),
-            pltpu.VMEM((slots, width, tile), bf16),
+            pltpu.VMEM((slots, 2 * width, tile), bf16),
             pltpu.VMEM((steps, n_col * TOUCH, width, tile), bf16),
             [pltpu.VMEM((n_col * TOUCH + 1, width, tile), bf16)] * steps,
             [pltpu.VMEM((n_row * BPD, width, tile), bf16)] * steps,
@@ -372,12 +412,12 @@
             pltpu.VMEM((8, slots), jnp.int32),
             pltpu.VMEM((n_col, 1, slots), jnp.int32),
             pltpu.VMEM((n_row, n_col, 1, slots), jnp.int32),
-            pltpu.VMEM((n_row * BPD, queries, tile), jnp.int32),
+            pltpu.VMEM((n_row * BPD, queries, tile), jnp.float32),
             pltpu.SMEM((8, slots), jnp.int32),
             pltpu.SMEM((n_row, n_col, 1, slots), jnp.int32),
             dma((CHUNKS,)), dma((n_col,)), dma((n_col,)), dma((n_row,)), dma((n_row,)), dma,
-            dma((steps,)), dma((steps,)),
-            dma((moves, 2 * n_row)), dma((moves, n_row)), dma((moves, n_row)),
+            dma, dma((steps,)),
+            dma((3,)), dma((moves, 2)),
         ],
         compiler_params=pltpu.CompilerParams(
             collective_id=0, has_side_effects=True, vmem_limit_bytes=60 * 1024 * 1024

time: 76.7 us -> 71.9 us (0.937)
  Pallas kernels: 74 us -> 69.2 us
    pallas_call x1, Pallas kernels: 74 us -> 69.2 us  [shards(): pl.pallas_call(functools.partial(katz_kernel, n_row, n_col), out_shape=ja...]
where the time goes in v2:
time: 71.9 us; the launch traced here: 71.7 us
  Pallas kernels  69.2 us (96%)
  local copies, waits for them, and re-layouts  1.87 us (3%)
    pallas_call x1, Pallas kernels, shards(): pl.pallas_call(functools.partial(katz_kernel, n_row, n_col), out_shape=ja...  69.2 us
    unnamed x1, local copies, waits for them, and re-layouts  1.87 us

profile of v2, /device:TPU:0, one launch (start us, length us, event | category | flops | bytes accessed | tf_op | source)
XLA Modules:
  0.0 71.7 jit_solution(11949206741050774481)
XLA Ops:
  0.7 69.2 %shard_map.64 = f32[1024,128]{1,0:T(8,128)} custom-call(s32[1,1]{1,0:T(1,128)S(6)} %copy.8.count_ref, s32[1,128]{1,0:T(1,128)} %bitcast.6, s32[1,128]{1,0:T(1,128)} %bitcast.7, s32[1,128]{1,0:T(1,128)} %bitcast.8, f32[1,128]{1,0:T(1,128)} %bitcast.9, bf16[128,128,128]{2,1,0:T(8,128)(2,1)} %bitcast.5), custom_call_target="tpu_custom_call" | custom-call | tf_op jit(solution)/shard_map/pallas_call | solution.py:396
  69.9 1.9 %copy.9 = f32[1024,128]{1,0:T(8,128)} copy(f32[1024,128]{1,0:T(8,128)} %shard_map.64) | data formatting | bytes 1048576
